TPU v7x, 256 devices: a 8x8x2 block of a 8x8x16 slice. The times are simulated.
256 devices in a mesh: groups: 2 (over z), roll: 16 (over y, core), rows: 8 (over x).
Axes of the slice: x: 8, y: 8, z: 2, core: 2. Of those that a mesh axis runs over, the one named last changes fastest.
The devices are a block of a 8x8x16 slice.
Arguments:
- latent_slabs: bfloat16 [64, 3, 64, 8, 16], P(('groups', 'roll'), None, 'rows'), parts along dimension 0, may hold values from -18 to 18, as said below
- prior_latents: bfloat16 [64, 2, 64, 8, 16], P(('groups', 'roll'), None, 'rows'), parts along dimension 0, may hold values from -6 to 6
- prior_features: bfloat16 [64, 2, 64, 8, 512], P(('groups', 'roll'), None, 'rows'), parts along dimension 0, may hold values from -6 to 6
- lengths: int32 [64], P(('groups', 'roll')), parts along dimension 0, may hold values from 1 to 3
- starts: int32 [64], P(('groups', 'roll')), parts along dimension 0, may hold values from 0 to 6, as said below
- move_plan: int32 [64], P(('groups', 'roll')), parts along dimension 0, may hold values from -1 to 15, as said below
- entry_weight: bfloat16 [432, 512], replicated, may hold values from -0.3125 to 0.3125
- block_weight: bfloat16 [13824, 512], P(None, ('roll', 'rows')), may hold values from -0.0546875 to 0.0546875
- norm_gain: float32 [512], replicated, may hold values from 0.25 to 1.75
- norm_shift: float32 [512], replicated, may hold values from -1.2 to 1.2
Outputs:
- decoded: bfloat16 [64, 3, 64, 8, 512], P(('groups', 'roll'), None, 'rows'), parts along dimension 0
There are 2 independent parts, one for each index of `groups`. A program takes and returns all parts, laid end to end along the dimension named above; an argument that names none is the same for every part. Nothing has to cross between parts.
Inputs may be any that keep to these rules, and one draw needn't show every extreme that they name: `latent_slabs`: normal or uniform values times a scale that varies over the rows. `starts`: multiples of 3. `move_plan`: A value d * 1 + c names compute slot c of roll index d. Every compute slot of the part is named by exactly one slab, and the slabs held by one roll index name at most 1 slots of any one roll index.
All inputs are finite; a program needn't handle non-finite values.
Results may differ from a plain program's by a relative error of at most 0.0023.
Values may be sent and summed in bfloat16 or wider, within the bound.
No kernel may reach another device: no remote copies, remote signals or barrier semaphores. Data moves between devices by JAX's collectives and lax.ppermute only.
A program may use at most 128 MiB of HBM per device.

v0:
```python
import jax
import jax.numpy as jnp
from jax import lax
from jax.sharding import PartitionSpec as P

GROUPS = 32
EPSILON = 1e-06


def padded(x, sides, width):
    for axis, dim in sides:
        count, length = (lax.axis_size(axis), x.shape[dim])
        up = [(i, (i + 1) % count) for i in range(count - 1)]
        down = [(j, i) for i, j in up]
        last = lax.slice_in_dim(x, length - width, length, axis=dim)
        first = lax.slice_in_dim(x, 0, width, axis=dim)
        before = lax.ppermute(last, axis, up)
        after = lax.ppermute(first, axis, down)
        x = jnp.concatenate([before, x, after], axis=dim)
    return x


def column_pad(extended):
    return jnp.pad(extended, ((0, 0), (0, 0), (0, 0), (1, 1), (0, 0)))


def convolve(extended, weights):
    slots = extended.shape[0]
    frames = extended.shape[1] - 2
    height = extended.shape[2] - 2
    widths = extended.shape[3] - 2
    channels = extended.shape[4]
    accumulated = jnp.zeros((slots * frames * height * widths, weights.shape[1]), jnp.float32)
    for tap_index in range(27):
        step_t = tap_index // 9
        step_h = tap_index // 3 % 3
        step_w = tap_index % 3
        window = extended[
            :, step_t : step_t + frames, step_h : step_h + height, step_w : step_w + widths, :
        ]
        accumulated = accumulated + jnp.dot(
            window.reshape(-1, channels),
            weights[tap_index * channels : (tap_index + 1) * channels],
            preferred_element_type=jnp.float32,
        )
    return accumulated.reshape(slots, frames, height, widths, weights.shape[1])


def decode(
    entry_ext, feature_cache, live_lengths, entry_weight, block_weight, norm_gain, norm_shift
):
    latent_rim = padded(entry_ext, (("rows", 2),), 1)
    hidden = convolve(column_pad(latent_rim), entry_weight)
    slots, frames, height, widths, features = hidden.shape
    grouped = hidden.reshape(slots, frames, height, widths, GROUPS, features // GROUPS)
    group_sums = jnp.sum(grouped, axis=(2, 3, 5))
    squares = jnp.sum(grouped * grouped, axis=(2, 3, 5))
    group_sums, squares = lax.psum((group_sums, squares), "rows")
    cell_count = height * lax.axis_size("rows") * widths * (features // GROUPS)
    group_mean = group_sums / cell_count
    spread = squares / cell_count - group_mean * group_mean
    scaled = lax.rsqrt(spread + EPSILON)
    normed = (
        (grouped - group_mean[:, :, None, None, :, None]) * scaled[:, :, None, None, :, None]
    ).reshape(hidden.shape)
    normed = normed * norm_gain + norm_shift
    active = jax.nn.silu(normed).astype(jnp.bfloat16)
    stacked = jnp.concatenate([feature_cache, active], axis=1)
    bordered = column_pad(padded(stacked, (("rows", 2),), 1))
    mixed_sum = convolve(
        bordered, lax.all_gather(block_weight, ("roll", "rows"), axis=1, tiled=True)
    )
    alive_frames = jnp.arange(frames)[None, :] < live_lengths[:, None]
    return jnp.where(alive_frames[:, :, None, None, None], hidden + mixed_sum, 0.0).astype(
        jnp.bfloat16
    )


def on_device(
    latent_slabs,
    prior_latents,
    prior_features,
    lengths,
    starts,
    move_plan,
    entry_weight,
    block_weight,
    norm_gain,
    norm_shift,
):
    cached = starts > 0
    prior_lat = jnp.where(
        cached[:, None, None, None, None], prior_latents, jnp.zeros_like(prior_latents)
    )
    feature_cache = jnp.where(
        cached[:, None, None, None, None], prior_features, jnp.zeros_like(prior_features)
    )
    entry_ext = jnp.concatenate([prior_lat, latent_slabs], axis=1)
    live_lengths = jnp.where(move_plan >= 0, lengths, 0)
    return decode(
        entry_ext, feature_cache, live_lengths, entry_weight, block_weight, norm_gain, norm_shift
    )


def solution(mesh):
    in_specs = (
        P(("groups", "roll"), None, "rows", None, None),
        P(("groups", "roll"), None, "rows", None, None),
        P(("groups", "roll"), None, "rows", None, None),
        P(("groups", "roll")),
        P(("groups", "roll")),
        P(("groups", "roll")),
        P(),
        P(None, ("roll", "rows")),
        P(),
        P(),
    )
    out_specs = P(("groups", "roll"), None, "rows", None, None)
    return jax.shard_map(
        on_device, mesh=mesh, in_specs=in_specs, out_specs=out_specs, check_vma=False
    )
```

profile of v0, /device:TPU:513, one launch (start us, length us, event | category | flops | bytes accessed | tf_op | source)
XLA Modules:
  0.0 172.0 jit_solution(16088518740461033009)
XLA Ops:
  9.6 1.3 collective-permute-start.1
  10.9 4.7 %collective-permute-start = (bf16[2,5,1,8,16]{4,3,2,1,0:T(8,128)(2,1)S(1)}, bf16[2,5,1,8,16]{4,3,2,1,0:T(8,128)(2,1)S(1)}, u32[]{:S(2)}, u32[]{:S(2)}) collective-permute-start(bf16[2,5,1,8,16]{4,3,2,1,0:T(8,128)(2,1)S(1)} %get-tuple-element.67), channel_id=1, source_target_pairs={{0,1},{1,2},{2,3},{3,4},{4,5},{5,6},{6,7},{8,9},{9,10},{10,11},{11... | collective-permute-start | bytes 7688 | tf_op jit(solution)/shard_map/ppermute | solution.py:17
  18.4 1.1 pad_maximum_fusion.2
  19.5 1.1 select_maximum_fusion.2
  31.0 4.1 %reshape_reshape.3 = f32[2,3,8,8,32,16]{5,4,3,2,1,0:T(8,128)} reshape(f32[384,512]{1,0:T(8,128)S(1)} %convolution_add_fusion.8) | data formatting | bytes 1572864 | tf_op jit(solution)/shard_map/reshape;reshape | solution.py:55
  35.1 4.0 %fusion.100 = (f32[2,3,32]{2,1,0:T(4,128)S(1)}, f32[2,3,32]{2,1,0:T(4,128)S(1)}) fusion(f32[2,3,8,8,32,16]{5,4,3,2,1,0:T(8,128)} %reshape_reshape.3), kind=kLoop, calls=%fused_computation.169 | loop fusion | flops 589440 | bytes 787968 | tf_op jit(solution)/shard_map/reduce_sum | solution.py:56
  39.1 14.4 %all-reduce.2 = (f32[2,3,32]{2,1,0:T(4,128)S(1)}, f32[2,3,32]{2,1,0:T(4,128)S(1)}) all-reduce(f32[2,3,32]{2,1,0:T(4,128)S(1)} %get-tuple-element.6, f32[2,3,32]{2,1,0:T(4,128)S(1)} %get-tuple-element.5), channel_id=1, replica_groups=mesh['groups'=2,'roll'=16,'rows'=8] {'rows'}, use_global_device_ids=true, to_apply=%region_3.4 | all-reduce | flops 384 | bytes 3072 | tf_op jit(solution)/shard_map/psum | solution.py:58
  55.3 2.2 %collective-permute-start.2 = (bf16[2,5,1,8,512]{4,3,2,1,0:T(8,128)(2,1)S(1)}, bf16[2,5,1,8,512]{4,3,2,1,0:T(8,128)(2,1)S(1)}, u32[]{:S(2)}, u32[]{:S(2)}) collective-permute-start(bf16[2,5,1,8,512]{4,3,2,1,0:T(8,128)(2,1)S(1)} %get-tuple-element.37), channel_id=1, source_target_pairs={{0,1},{1,2},{2,3},{3,4},{4,5},{5,6},{6,7},{8,9},{9,10},{10,11},{11... | collective-permute-start | bytes 245768 | tf_op jit(solution)/shard_map/ppermute | solution.py:17
  57.5 1.5 collective-permute-start.3
  60.0 3.6 %collective-permute-done.3 = bf16[2,5,1,8,512]{4,3,2,1,0:T(8,128)(2,1)S(1)} collective-permute-done((bf16[2,5,1,8,512]{4,3,2,1,0:T(8,128)(2,1)S(1)}, bf16[2,5,1,8,512]{4,3,2,1,0:T(8,128)(2,1)S(1)}, u32[]{:S(2)}, u32[]{:S(2)}) %collective-permute-start.3) | collective-permute-done | bytes 81952 | tf_op jit(solution)/shard_map/ppermute | solution.py:18
  63.7 1.0 fusion.103
  64.8 1.1 fusion.102
  66.8 2.5 %fusion.101 = (bf16[2,3,8,8,512]{4,3,2,1,0:T(8,128)(2,1)S(1)}, bf16[2,3,8,8,512]{4,3,2,1,0:T(8,128)(2,1)}, bf16[2,3,8,8,512]{4,3,2,1,0:T(8,128)(2,1)}, bf16[2,3,...) fusion(bf16[2,5,10,10,512]{4,3,2,1,0:T(8,128)(2,1)S(1)} %select, ...), kind=kLoop, calls=%fused_computation.170 | loop fusion | bytes 14155776 | tf_op jit(solution)/shard_map/slice | solution.py:38
  69.3 51.0 %all-gather.3.cloned.1.call-done = bf16[128,4,13824]{2,1,0:T(4,128)(2,1)} async-done(((bf16[1,4,13824]{2,1,0:T(4,128)(2,1)}), bf16[128,4,13824]{2,1,0:T(4,128)(2,1)}) %all-gather.3.cloned.1.call-update) | async-done | bytes 14155792 | tf_op jit(solution)/shard_map/all_gather | solution.py:71
  120.3 20.3 %reshape.254 = bf16[512,13824]{1,0:T(8,128)(2,1)} reshape(bf16[128,4,13824]{2,1,0:T(4,128)(2,1)} %all-gather.3.cloned.1.call-done) | data formatting | bytes 28311552
  140.7 1.7 fusion.22
  142.4 2.3 %fusion.24 = f32[384,512]{1,0:T(8,128)S(1)} fusion(bf16[384,512]{1,0:T(8,128)(2,1)} %bitcast.177, bf16[13824,512]{0,1:T(8,128)(2,1)} %bitcast.136), kind=kOutput, calls=%fused_computation.74 | convolution fusion | flops 201326592 | bytes 1703936 | tf_op jit(solution)/shard_map/dot_general | solution.py:41
  144.7 2.3 %fusion.27 = f32[384,512]{1,0:T(8,128)S(1)} fusion(bf16[384,512]{1,0:T(8,128)(2,1)} %multiply_convert_fusion, bf16[13824,512]{0,1:T(8,128)(2,1)} %bitcast.137), kind=kOutput, calls=%fused_computation.77 | convolution fusion | flops 201326592 | bytes 1703936 | tf_op jit(solution)/shard_map/dot_general | solution.py:41
  147.0 1.6 fusion.29
  148.6 1.6 fusion.32
  150.2 1.6 fusion.34
  151.7 1.6 fusion.37
  153.3 1.6 fusion.39
  154.9 1.6 fusion.42
  (107 shorter events, 28.0 us)
Async XLA Ops:
  6.5 19.2 %copy-start.13 = (bf16[432,512]{1,0:T(8,128)(2,1)S(1)}, bf16[432,512]{1,0:T(8,128)(2,1)}, u32[]{:S(2)}) copy-start(bf16[432,512]{1,0:T(8,128)(2,1)} %param.16) | copy-start | bytes 1327108
  6.5 113.8 %all-gather.3.cloned.1.call-start = ((), (), s32[]{:S(2)}) async-start(), calls=%async_computation | async-start | bytes 14266368 | tf_op jit(solution)/shard_map/all_gather | solution.py:71
  9.6 8.8 %collective-permute-start.1 = (bf16[2,5,1,8,16]{4,3,2,1,0:T(8,128)(2,1)S(1)}, bf16[2,5,1,8,16]{4,3,2,1,0:T(8,128)(2,1)S(1)}, u32[]{:S(2)}, u32[]{:S(2)}) collective-permute-start(bf16[2,5,1,8,16]{4,3,2,1,0:T(8,128)(2,1)S(1)} %get-tuple-element.68), channel_id=1, source_target_pairs={{1,0},{2,1},{3,2},{4,3},{5,4},{6,5},{7,6},{9,8},{10,9},{11,10},{12... | collective-permute-start | bytes 7688 | tf_op jit(solution)/shard_map/ppermute | solution.py:18
  10.9 7.4 %collective-permute-start = (bf16[2,5,1,8,16]{4,3,2,1,0:T(8,128)(2,1)S(1)}, bf16[2,5,1,8,16]{4,3,2,1,0:T(8,128)(2,1)S(1)}, u32[]{:S(2)}, u32[]{:S(2)}) collective-permute-start(bf16[2,5,1,8,16]{4,3,2,1,0:T(8,128)(2,1)S(1)} %get-tuple-element.67), channel_id=1, source_target_pairs={{0,1},{1,2},{2,3},{3,4},{4,5},{5,6},{6,7},{8,9},{9,10},{10,11},{11... | collective-permute-start | bytes 7688 | tf_op jit(solution)/shard_map/ppermute | solution.py:17
  25.8 4.0 %copy-start.1 = (bf16[2,3,8,8,16]{4,3,2,1,0:T(8,128)(2,1)S(1)}, bf16[2,3,8,8,16]{4,3,2,1,0:T(8,128)(2,1)}, u32[]{:S(2)}) copy-start(bf16[2,3,8,8,16]{4,3,2,1,0:T(8,128)(2,1)} %param.10) | copy-start | bytes 36868
  28.8 25.2 %copy-start.14 = (f32[512]{0:T(512)S(1)}, f32[512]{0:T(512)}, u32[]{:S(2)}) copy-start(f32[512]{0:T(512)} %param.19) | copy-start | bytes 6148
  28.8 25.2 %copy-start.15 = (f32[512]{0:T(512)S(1)}, f32[512]{0:T(512)}, u32[]{:S(2)}) copy-start(f32[512]{0:T(512)} %param.18) | copy-start | bytes 6148
  55.3 4.6 %collective-permute-start.2 = (bf16[2,5,1,8,512]{4,3,2,1,0:T(8,128)(2,1)S(1)}, bf16[2,5,1,8,512]{4,3,2,1,0:T(8,128)(2,1)S(1)}, u32[]{:S(2)}, u32[]{:S(2)}) collective-permute-start(bf16[2,5,1,8,512]{4,3,2,1,0:T(8,128)(2,1)S(1)} %get-tuple-element.37), channel_id=1, source_target_pairs={{0,1},{1,2},{2,3},{3,4},{4,5},{5,6},{6,7},{8,9},{9,10},{10,11},{11... | collective-permute-start | bytes 245768 | tf_op jit(solution)/shard_map/ppermute | solution.py:17
  57.5 6.1 %collective-permute-start.3 = (bf16[2,5,1,8,512]{4,3,2,1,0:T(8,128)(2,1)S(1)}, bf16[2,5,1,8,512]{4,3,2,1,0:T(8,128)(2,1)S(1)}, u32[]{:S(2)}, u32[]{:S(2)}) collective-permute-start(bf16[2,5,1,8,512]{4,3,2,1,0:T(8,128)(2,1)S(1)} %get-tuple-element.38), channel_id=1, source_target_pairs={{1,0},{2,1},{3,2},{4,3},{5,4},{6,5},{7,6},{9,8},{10,9},{11,10},{12... | collective-permute-start | bytes 245768 | tf_op jit(solution)/shard_map/ppermute | solution.py:18
  140.6 15.8 %copy-start = (bf16[512,13824]{1,0:T(8,128)(2,1)S(1)}, bf16[512,13824]{1,0:T(8,128)(2,1)}, u32[]{:S(2)}) copy-start(bf16[512,13824]{1,0:T(8,128)(2,1)} %reshape.254) | copy-start | bytes 42467332
  140.6 15.8 %copy-start.2 = (bf16[2,3,8,8,512]{4,3,2,1,0:T(8,128)(2,1)S(1)}, bf16[2,3,8,8,512]{4,3,2,1,0:T(8,128)(2,1)}, u32[]{:S(2)}) copy-start(bf16[2,3,8,8,512]{4,3,2,1,0:T(8,128)(2,1)} %get-tuple-element.18) | copy-start | bytes 1179652
  140.6 16.3 %copy-start.11 = (bf16[2,3,8,8,512]{4,3,2,1,0:T(8,128)(2,1)S(1)}, bf16[2,3,8,8,512]{4,3,2,1,0:T(8,128)(2,1)}, u32[]{:S(2)}) copy-start(bf16[2,3,8,8,512]{4,3,2,1,0:T(8,128)(2,1)} %get-tuple-element.29) | copy-start | bytes 1179652
  140.6 17.1 %copy-start.10 = (bf16[2,3,8,8,512]{4,3,2,1,0:T(8,128)(2,1)S(1)}, bf16[2,3,8,8,512]{4,3,2,1,0:T(8,128)(2,1)}, u32[]{:S(2)}) copy-start(bf16[2,3,8,8,512]{4,3,2,1,0:T(8,128)(2,1)} %get-tuple-element.30) | copy-start | bytes 1179652
  140.7 17.9 %copy-start.12 = (bf16[2,3,8,8,512]{4,3,2,1,0:T(8,128)(2,1)S(1)}, bf16[2,3,8,8,512]{4,3,2,1,0:T(8,128)(2,1)}, u32[]{:S(2)}) copy-start(bf16[2,3,8,8,512]{4,3,2,1,0:T(8,128)(2,1)} %get-tuple-element.33) | copy-start | bytes 1179652
  142.4 17.8 %copy-start.9 = (bf16[2,3,8,8,512]{4,3,2,1,0:T(8,128)(2,1)S(1)}, bf16[2,3,8,8,512]{4,3,2,1,0:T(8,128)(2,1)}, u32[]{:S(2)}) copy-start(bf16[2,3,8,8,512]{4,3,2,1,0:T(8,128)(2,1)} %get-tuple-element.27) | copy-start | bytes 1179652
  153.3 7.9 %copy-start.8 = (bf16[2,3,8,8,512]{4,3,2,1,0:T(8,128)(2,1)S(1)}, bf16[2,3,8,8,512]{4,3,2,1,0:T(8,128)(2,1)}, u32[]{:S(2)}) copy-start(bf16[2,3,8,8,512]{4,3,2,1,0:T(8,128)(2,1)} %get-tuple-element.21) | copy-start | bytes 1179652
  156.5 5.1 %copy-start.7 = (bf16[2,3,8,8,512]{4,3,2,1,0:T(8,128)(2,1)S(1)}, bf16[2,3,8,8,512]{4,3,2,1,0:T(8,128)(2,1)}, u32[]{:S(2)}) copy-start(bf16[2,3,8,8,512]{4,3,2,1,0:T(8,128)(2,1)} %get-tuple-element.19) | copy-start | bytes 1179652
  157.3 4.7 %copy-start.6 = (bf16[2,3,8,8,512]{4,3,2,1,0:T(8,128)(2,1)S(1)}, bf16[2,3,8,8,512]{4,3,2,1,0:T(8,128)(2,1)}, u32[]{:S(2)}) copy-start(bf16[2,3,8,8,512]{4,3,2,1,0:T(8,128)(2,1)} %get-tuple-element.17) | copy-start | bytes 1179652
  158.5 3.9 %copy-start.5 = (bf16[2,3,8,8,512]{4,3,2,1,0:T(8,128)(2,1)S(1)}, bf16[2,3,8,8,512]{4,3,2,1,0:T(8,128)(2,1)}, u32[]{:S(2)}) copy-start(bf16[2,3,8,8,512]{4,3,2,1,0:T(8,128)(2,1)} %get-tuple-element.15) | copy-start | bytes 1179652
  159.4 3.6 %copy-start.4 = (bf16[2,3,8,8,512]{4,3,2,1,0:T(8,128)(2,1)S(1)}, bf16[2,3,8,8,512]{4,3,2,1,0:T(8,128)(2,1)}, u32[]{:S(2)}) copy-start(bf16[2,3,8,8,512]{4,3,2,1,0:T(8,128)(2,1)} %get-tuple-element.13) | copy-start | bytes 1179652
  160.6 2.8 %copy-start.3 = (bf16[2,3,8,8,512]{4,3,2,1,0:T(8,128)(2,1)S(1)}, bf16[2,3,8,8,512]{4,3,2,1,0:T(8,128)(2,1)}, u32[]{:S(2)}) copy-start(bf16[2,3,8,8,512]{4,3,2,1,0:T(8,128)(2,1)} %get-tuple-element.11) | copy-start | bytes 1179652
Sparse Core Ops, SparseCore 0:
  10.0 110.3 all-gather.2
where the time goes:
time: 173 us; the launch traced here: 172 us
  waiting for transfers between devices  55.4 us (32%)
  matrix products  32.9 us (19%)
  local copies, waits for them, and re-layouts  29.9 us (17%)
  other arithmetic  15.4 us (9%)
  blocking collectives  14.4 us (8%)
  between operations  14.2 us (8%)
  starting transfers between devices  9.74 us (6%)
    all_gather x1, waiting for transfers between devices, decode(): lax.all_gather(block_weight, ('roll', 'rows'), axis=1, tiled=True)  51 us
    dot_general x54, matrix products, convolve(): jnp.dot(window.reshape(-1, channels), weights[tap_index * channels:(tap_i...  32.9 us
    unnamed x33, local copies, waits for them, and re-layouts  20.4 us
    psum x1, blocking collectives, decode(): group_sums, squares = lax.psum((group_sums, squares), 'rows')  14.4 us
    ppermute x2, starting transfers between devices, padded(): before = lax.ppermute(last, axis, up)  6.94 us
    slice x5, local copies, waits for them, and re-layouts, convolve(): extended[:, step_t:step_t + frames, step_h:step_h + height, step_w:step_w...  5.04 us
    another operation x1, local copies, waits for them, and re-layouts, decode(): hidden.reshape(slots, frames, height, widths, GROUPS, features // GROUPS)  4.1 us
    reduce_sum x1, other arithmetic, decode(): group_sums = jnp.sum(grouped, axis=(2, 3, 5))  4.05 us
  transfers between devices with their start and end apart: 5, of which 2 were waited for; matrix products, arithmetic and copies ran while one was open for 20% of the time, Pallas kernels for 0%

commit v1 on v0

--- a/solution.py
+++ b/solution.py
@@ -67,9 +67,16 @@
     active = jax.nn.silu(normed).astype(jnp.bfloat16)
     stacked = jnp.concatenate([feature_cache, active], axis=1)
     bordered = column_pad(padded(stacked, (("rows", 2),), 1))
-    mixed_sum = convolve(
-        bordered, lax.all_gather(block_weight, ("roll", "rows"), axis=1, tiled=True)
+    feed_lines_on_mesh = lambda frame, axis_no: jnp.concatenate(
+        lax.all_to_all(
+            jnp.stack(lax.psum(1, axis_name=("roll", "rows")) * [frame], axis=0),
+            axis_name=("roll", "rows"),
+            concat_axis=0,
+            split_axis=0,
+        ),
+        axis_no,
     )
+    mixed_sum = convolve(bordered, feed_lines_on_mesh(block_weight, 1))
     alive_frames = jnp.arange(frames)[None, :] < live_lengths[:, None]
     return jnp.where(alive_frames[:, :, None, None, None], hidden + mixed_sum, 0.0).astype(
         jnp.bfloat16

time: 173 us -> 608 us (3.51)
  the two profiles are of different devices: /device:TPU:513 before, /device:TPU:582 now
where the time goes in v1:
time: 608 us; the launch traced here: 607 us
  waiting for transfers between devices  397 us (65%)
  local copies, waits for them, and re-layouts  75.7 us (12%)
  blocking collectives  65.8 us (11%)
  starting transfers between devices  37.3 us (6%)
  matrix products  20.7 us (3%)
  other arithmetic  8.86 us (1%)
    ppermute x2, waiting for transfers between devices, padded(): before = lax.ppermute(last, axis, up)  388 us
    psum x1, blocking collectives, decode(): group_sums, squares = lax.psum((group_sums, squares), 'rows')  65.8 us
    slice x29, local copies, waits for them, and re-layouts, convolve(): weights[tap_index * channels:(tap_index + 1) * channels]  57.6 us
    all_to_all x1, starting transfers between devices, decode(): lax.all_to_all(jnp.stack(lax.psum(1, axis_name=('roll', 'rows')) * [frame...  23.2 us
    dot_general x54, matrix products, convolve(): jnp.dot(window.reshape(-1, channels), weights[tap_index * channels:(tap_i...  20.7 us
  transfers between devices with their start and end apart: 5, of which 3 were waited for; matrix products, arithmetic and copies ran while one was open for 4% of the time, Pallas kernels for 0%

profile of v1, /device:TPU:582, one launch (start us, length us, event | category | flops | bytes accessed | tf_op | source)
XLA Modules:
  0.0 606.6 jit_solution(12398387337412590054)
XLA Ops:
  0.0 6.1 stack.2
  6.1 23.2 %all-to-all-start = ((bf16[128,13824,4]{1,2,0:T(4,128)(2,1)}), bf16[128,13824,4]{1,2,0:T(4,128)(2,1)}, u32[]{:S(2)}, u32[]{:S(2)}) async-start(bf16[128,13824,4]{1,2,0:T(4,128)(2,1)} %stack.2), calls=%async_computation | async-start | bytes 28311552 | tf_op jit(solution)/shard_map/all_to_all | solution.py:71
  29.4 4.6 collective-permute-start
  36.3 387.7 %collective-permute-done = bf16[2,5,1,8,16]{4,3,2,1,0:T(8,128)(2,1)S(1)} collective-permute-done((bf16[2,5,1,8,16]{4,3,2,1,0:T(8,128)(2,1)S(1)}, bf16[2,5,1,8,16]{4,3,2,1,0:T(8,128)(2,1)S(1)}, u32[]{:S(2)}, u32[]{:S(2)}) %collective-permute-start) | collective-permute-done | bytes 2592 | tf_op jit(solution)/shard_map/ppermute | solution.py:17
  423.9 4.9 collective-permute-done.1
  435.8 4.1 reshape_reshape.3
  439.9 4.1 fusion.54
  443.9 65.8 %all-reduce.2 = (f32[2,3,32]{2,1,0:T(4,128)S(1)}, f32[2,3,32]{2,1,0:T(4,128)S(1)}) all-reduce(f32[2,3,32]{2,1,0:T(4,128)S(1)} %get-tuple-element.6, f32[2,3,32]{2,1,0:T(4,128)S(1)} %get-tuple-element.5), channel_id=1, replica_groups=mesh['groups'=2,'roll'=16,'rows'=8] {'rows'}, use_global_device_ids=true, to_apply=%region_3.4 | all-reduce | flops 384 | bytes 3072 | tf_op jit(solution)/shard_map/psum | solution.py:58
  511.6 5.4 collective-permute-start.2
  517.0 2.1 collective-permute-start.3
  520.1 4.5 collective-permute-done.3
  527.7 3.2 fusion.57
  530.9 4.0 fusion.56
  535.0 8.0 %fusion.55 = (bf16[512,128,4]{0,2,1:T(4,128)(2,1)S(1)}, bf16[512,128,4]{0,2,1:T(4,128)(2,1)S(1)}, bf16[512,128,4]{0,2,1:T(4,128)(2,1)S(1)}, bf16[512,128,4]{0,2,...) fusion(bf16[13824,128,4]{0,2,1:T(4,128)(2,1)} %bitcast.29), kind=kLoop, calls=%fused_computation.124 | loop fusion | bytes 19922944 | tf_op jit(solution)/shard_map/slice | solution.py:43
  543.0 2.0 slice.508
  545.0 2.0 slice.514
  548.9 2.0 slice.526
  550.9 2.0 slice.511
  556.9 2.0 slice.535
  560.9 2.0 slice.532
  564.8 2.0 slice.547
  568.8 2.0 slice.553
  578.6 2.0 slice.559
  580.6 2.0 slice.571
  (211 shorter events, 57.9 us)
Async XLA Ops:
  6.1 23.2 %copy-start.51 = (s32[2]{0:T(128)S(1)}, s32[2]{0:T(128)}, u32[]{:S(2)}) copy-start(s32[2]{0:T(128)} %param.14) | copy-start | bytes 28
  6.1 23.2 %copy-start.48 = (bf16[2,2,8,8,16]{4,3,2,1,0:T(8,128)(2,1)S(1)}, bf16[2,2,8,8,16]{4,3,2,1,0:T(8,128)(2,1)}, u32[]{:S(2)}) copy-start(bf16[2,2,8,8,16]{4,3,2,1,0:T(8,128)(2,1)} %param.11) | copy-start | bytes 24580
  6.1 23.3 %copy-start = (bf16[2,3,8,8,16]{4,3,2,1,0:T(8,128)(2,1)S(1)}, bf16[2,3,8,8,16]{4,3,2,1,0:T(8,128)(2,1)}, u32[]{:S(2)}) copy-start(bf16[2,3,8,8,16]{4,3,2,1,0:T(8,128)(2,1)} %param.10) | copy-start | bytes 36868
  6.1 29.9 %copy-start.52 = (s32[2]{0:T(128)S(1)}, s32[2]{0:T(128)}, u32[]{:S(2)}) copy-start(s32[2]{0:T(128)} %param.13) | copy-start | bytes 28
  6.1 29.9 %copy-start.53 = (s32[2]{0:T(128)S(1)}, s32[2]{0:T(128)}, u32[]{:S(2)}) copy-start(s32[2]{0:T(128)} %param.15) | copy-start | bytes 28
  6.1 30.0 %copy-start.47 = (bf16[2,2,8,8,512]{4,3,2,1,0:T(8,128)(2,1)S(1)}, bf16[2,2,8,8,512]{4,3,2,1,0:T(8,128)(2,1)}, u32[]{:S(2)}) copy-start(bf16[2,2,8,8,512]{4,3,2,1,0:T(8,128)(2,1)} %param.12) | copy-start | bytes 786436
  6.1 524.8 %all-to-all-start = ((bf16[128,13824,4]{1,2,0:T(4,128)(2,1)}), bf16[128,13824,4]{1,2,0:T(4,128)(2,1)}, u32[]{:S(2)}, u32[]{:S(2)}) async-start(bf16[128,13824,4]{1,2,0:T(4,128)(2,1)} %stack.2), calls=%async_computation | async-start | bytes 28311552 | tf_op jit(solution)/shard_map/all_to_all | solution.py:71
  29.4 394.5 %collective-permute-start = (bf16[2,5,1,8,16]{4,3,2,1,0:T(8,128)(2,1)S(1)}, bf16[2,5,1,8,16]{4,3,2,1,0:T(8,128)(2,1)S(1)}, u32[]{:S(2)}, u32[]{:S(2)}) collective-permute-start(bf16[2,5,1,8,16]{4,3,2,1,0:T(8,128)(2,1)S(1)} %get-tuple-element.94), channel_id=1, source_target_pairs={{0,1},{1,2},{2,3},{3,4},{4,5},{5,6},{6,7},{8,9},{9,10},{10,11},{11... | collective-permute-start | bytes 7688 | tf_op jit(solution)/shard_map/ppermute | solution.py:17
  34.1 394.7 %collective-permute-start.1 = (bf16[2,5,1,8,16]{4,3,2,1,0:T(8,128)(2,1)S(1)}, bf16[2,5,1,8,16]{4,3,2,1,0:T(8,128)(2,1)S(1)}, u32[]{:S(2)}, u32[]{:S(2)}) collective-permute-start(bf16[2,5,1,8,16]{4,3,2,1,0:T(8,128)(2,1)S(1)} %get-tuple-element.95), channel_id=1, source_target_pairs={{1,0},{2,1},{3,2},{4,3},{5,4},{6,5},{7,6},{9,8},{10,9},{11,10},{12... | collective-permute-start | bytes 7688 | tf_op jit(solution)/shard_map/ppermute | solution.py:18
  36.1 393.4 %copy-start.46 = (bf16[432,512]{1,0:T(8,128)(2,1)S(1)}, bf16[432,512]{1,0:T(8,128)(2,1)}, u32[]{:S(2)}) copy-start(bf16[432,512]{1,0:T(8,128)(2,1)} %param.16) | copy-start | bytes 1327108
  439.9 70.4 %copy-start.49 = (f32[512]{0:T(512)S(1)}, f32[512]{0:T(512)}, u32[]{:S(2)}) copy-start(f32[512]{0:T(512)} %param.19) | copy-start | bytes 6148
  439.9 70.4 %copy-start.50 = (f32[512]{0:T(512)S(1)}, f32[512]{0:T(512)}, u32[]{:S(2)}) copy-start(f32[512]{0:T(512)} %param.18) | copy-start | bytes 6148
  511.6 8.5 %collective-permute-start.2 = (bf16[2,5,1,8,512]{4,3,2,1,0:T(8,128)(2,1)S(1)}, bf16[2,5,1,8,512]{4,3,2,1,0:T(8,128)(2,1)S(1)}, u32[]{:S(2)}, u32[]{:S(2)}) collective-permute-start(bf16[2,5,1,8,512]{4,3,2,1,0:T(8,128)(2,1)S(1)} %get-tuple-element.64), channel_id=1, source_target_pairs={{0,1},{1,2},{2,3},{3,4},{4,5},{5,6},{6,7},{8,9},{9,10},{10,11},{11... | collective-permute-start | bytes 245768 | tf_op jit(solution)/shard_map/ppermute | solution.py:17
  517.0 7.6 %collective-permute-start.3 = (bf16[2,5,1,8,512]{4,3,2,1,0:T(8,128)(2,1)S(1)}, bf16[2,5,1,8,512]{4,3,2,1,0:T(8,128)(2,1)S(1)}, u32[]{:S(2)}, u32[]{:S(2)}) collective-permute-start(bf16[2,5,1,8,512]{4,3,2,1,0:T(8,128)(2,1)S(1)} %get-tuple-element.65), channel_id=1, source_target_pairs={{1,0},{2,1},{3,2},{4,3},{5,4},{6,5},{7,6},{9,8},{10,9},{11,10},{12... | collective-permute-start | bytes 245768 | tf_op jit(solution)/shard_map/ppermute | solution.py:18
  588.6 3.4 copy-start.15
  588.6 3.4 copy-start.30
  588.6 5.5 copy-start.12
  588.6 5.5 copy-start.41
  590.3 4.2 copy-start.8
  590.3 4.2 copy-start.42
  592.0 3.0 copy-start.3
  592.0 3.0 copy-start.45
  592.4 3.0 copy-start.13
  592.4 3.0 copy-start.29
  (35 other events, 53.2 us)
